TPU v7x, 32 devices: a whole 2x2x4 slice. The times are simulated.
32 devices in a mesh: seq: 8 (over z, x), tensor: 4 (over y, core).
Axes of the slice: x: 2, y: 2, z: 4, core: 2. Of those that a mesh axis runs over, the one named last changes fastest.
Arguments:
- tokens: bfloat16 [4096, 2048], P('seq', 'tensor'), may hold values from -12 to 12
- attn_gain: float32 [2048], replicated, may hold values from 0.1 to 1.9
- w_query: bfloat16 [2048, 2048], P('seq', 'tensor'), as said below
- w_key: bfloat16 [2048, 512], P('seq', 'tensor'), as said below
- w_value: bfloat16 [2048, 512], P('seq', 'tensor'), may hold values from -0.125 to 0.125
- w_out: bfloat16 [2048, 2048], P('tensor', 'seq'), may hold values from -0.125 to 0.125
- mlp_gain: float32 [2048], replicated, may hold values from 0.1 to 1.9
- w_gate: bfloat16 [2048, 5632], P('seq', 'tensor'), may hold values from -0.125 to 0.125
- w_up: bfloat16 [2048, 5632], P('seq', 'tensor'), may hold values from -0.125 to 0.125
- w_down: bfloat16 [5632, 2048], P('tensor', 'seq'), may hold values from -0.078125 to 0.078125
Outputs:
- layer_out: bfloat16 [4096, 2048], P('seq', 'tensor')
Inputs may be any that keep to these rules, and one draw needn't show every extreme that they name: `w_query`: entries are of order 2048 to the power -1/2. `w_key`: entries are of order 2048 to the power -1/2.
All inputs are finite; a program needn't handle non-finite values.
Results may differ from a plain program's by a relative error of at most 0.013.
Values may be sent and summed in bfloat16 or wider, within the bound.
A program may use at most 128 MiB of HBM per device.

v0:
```python
import jax
import jax.numpy as jnp
from jax import lax
from jax.sharding import PartitionSpec as P

HEAD_DIM = 128
WINDOW = 1024


def passed_along(block, axis, distance):
    devices = range(lax.axis_size(axis))
    route = [(i - distance, i) for i in devices if i - distance in devices]
    return lax.ppermute(block, axis, route)


def scaled_rows(values, gain):
    values = values.astype(jnp.float32)
    mean_square = jnp.mean(values * values, axis=1, keepdims=True)
    return (values * lax.rsqrt(mean_square + 1e-06) * gain).astype(jnp.bfloat16)


def product(left, right):
    return jnp.dot(left, right, preferred_element_type=jnp.float32)


def window_attention(queries, context_keys, context_values, reach, position):
    rows = queries.shape[0]
    local_kv = context_keys.shape[1] // HEAD_DIM
    group = queries.shape[1] // (local_kv * HEAD_DIM)
    block = min(512, rows)
    span = WINDOW + block
    scale = HEAD_DIM ** (-0.5)
    start = reach * rows - WINDOW
    query_block = queries.reshape(block, local_kv, group, HEAD_DIM)
    key_block = context_keys.reshape(span, local_kv, HEAD_DIM)
    value_block = context_values.reshape(span, local_kv, HEAD_DIM)
    scores = (
        jnp.einsum("qkgd,ckd->kgqc", query_block, key_block, preferred_element_type=jnp.float32)
        * scale
    )
    query_pos = lax.broadcasted_iota(jnp.int32, (block, span), 0)
    key_pos = lax.broadcasted_iota(jnp.int32, (block, span), 1)
    distance = query_pos + WINDOW - key_pos
    first_key = (position - reach) * rows + start
    allowed = (distance >= 0) & (distance < WINDOW) & (key_pos + first_key >= 0)
    scores = jnp.where(allowed[None, None], scores, -1e30)
    highest = jnp.max(scores, axis=3, keepdims=True)
    raised = jnp.exp(scores - highest)
    weights = (raised / jnp.sum(raised, axis=3, keepdims=True)).astype(jnp.bfloat16)
    mixed = jnp.einsum("kgqc,ckd->qkgd", weights, value_block, preferred_element_type=jnp.float32)
    outputs = mixed.astype(jnp.bfloat16).reshape(block, local_kv * group * HEAD_DIM)
    return outputs


def per_device(tokens, attn_gain, w_query, w_key, w_value, w_out, mlp_gain, w_gate, w_up, w_down):
    rows = tokens.shape[0]
    whole = lax.all_gather(tokens, "tensor", axis=1, tiled=True)
    normed = scaled_rows(whole, attn_gain)
    query_full = lax.all_gather(w_query, "seq", axis=0, tiled=True)
    key_full, value_full = (
        lax.all_gather(w_key, "seq", axis=0, tiled=True),
        lax.all_gather(w_value, "seq", axis=0, tiled=True),
    )
    queries = product(normed, query_full).astype(jnp.bfloat16)
    keys = product(normed, key_full).astype(jnp.bfloat16)
    values = product(normed, value_full).astype(jnp.bfloat16)
    reach = -(-WINDOW // rows)
    earlier = []
    for step in range(reach):
        earlier.append(passed_along((keys, values), "seq", step + 1))
    context_keys = jnp.concatenate(
        [earlier[reach - 1 - step][0] for step in range(reach)] + [keys], axis=0
    )
    context_values = jnp.concatenate(
        [earlier[reach - 1 - step][1] for step in range(reach)] + [values], axis=0
    )
    position = lax.axis_index("seq")
    attended = window_attention(queries, context_keys, context_values, reach, position)
    out_full = lax.all_gather(w_out, "seq", axis=1, tiled=True)
    head_terms = product(attended, out_full)
    share = tokens.shape[1]
    attn_whole = lax.psum(head_terms.astype(jnp.bfloat16), "tensor").astype(jnp.float32)
    stream_whole = (whole.astype(jnp.float32) + attn_whole).astype(jnp.bfloat16)
    stream_share = lax.dynamic_slice_in_dim(
        stream_whole, lax.axis_index("tensor") * share, share, 1
    )
    stream_normed = scaled_rows(stream_whole, mlp_gain)
    gate_full = lax.all_gather(w_gate, "seq", axis=0, tiled=True)
    up_full = lax.all_gather(w_up, "seq", axis=0, tiled=True)
    gate = product(stream_normed, gate_full)
    upward = product(stream_normed, up_full)
    hidden = (jax.nn.silu(gate) * upward).astype(jnp.bfloat16)
    down_full = lax.all_gather(w_down, "seq", axis=1, tiled=True)
    unit_terms = product(hidden, down_full)
    mlp_share = lax.psum_scatter(
        unit_terms.astype(jnp.bfloat16), "tensor", scatter_dimension=1, tiled=True
    ).astype(jnp.float32)
    return (stream_share.astype(jnp.float32) + mlp_share).astype(jnp.bfloat16)


def solution(mesh):
    in_specs = (
        P("seq", "tensor"),
        P(),
        P("seq", "tensor"),
        P("seq", "tensor"),
        P("seq", "tensor"),
        P("tensor", "seq"),
        P(),
        P("seq", "tensor"),
        P("seq", "tensor"),
        P("tensor", "seq"),
    )
    out_specs = P("seq", "tensor")
    return jax.shard_map(
        per_device, mesh=mesh, in_specs=in_specs, out_specs=out_specs, check_vma=False
    )
```

profile of v0, /device:TPU:0, one launch (start us, length us, event | category | flops | bytes accessed | tf_op | source)
XLA Modules:
  0.0 529.0 jit_solution(15447656682437301794)
XLA Ops:
  6.5 0.7 all-gather.7.cloned.1.call-update
  7.3 0.0 all-gather.9.cloned.1.call-start
  7.3 0.7 all-gather.9.cloned.1.call-update
  8.0 0.0 all-gather.11.cloned.1.call-start
  8.1 0.7 all-gather.11.cloned.1.call-update
  8.7 0.0 all-reduce.2.cloned.1.call-start
  8.8 33.4 %all_gather.26 = bf16[2048,128]{1,0:T(8,128)(2,1)S(1)} all-gather(bf16[256,128]{1,0:T(8,128)(2,1)} %param.13), channel_id=1, replica_groups=mesh['seq'=8,'tensor'=4] {'seq'}, dimensions={0}, use_global_device_ids=true | all-gather | bytes 589824 | tf_op jit(solution)/shard_map/all_gather | solution.py:61
  42.2 35.2 %all_gather.25 = bf16[2048,128]{1,0:T(8,128)(2,1)} all-gather(bf16[256,128]{1,0:T(8,128)(2,1)} %param.14), channel_id=1, replica_groups=mesh['seq'=8,'tensor'=4] {'seq'}, dimensions={0}, use_global_device_ids=true | all-gather | bytes 589824 | tf_op jit(solution)/shard_map/all_gather | solution.py:62
  77.3 1.3 fusion.14
  78.6 0.0 all-gather.7.cloned.1.call-done
  78.7 2.2 fusion.7
  80.9 2.4 convolution_convert_fusion.3
  83.3 1.3 collective-permute-start.2
  84.6 4.3 collective-permute-start.3
  88.9 0.8 convolution_convert_fusion.4
  89.6 2.7 collective-permute-start
  92.4 2.7 collective-permute-start.1
  95.1 0.0 all-gather.9.cloned.1.call-done
  95.1 3.0 convolution_convert_fusion.2
  98.1 0.0 collective-permute-done.2
  98.1 0.0 collective-permute-done.3
  98.1 3.3 fusion.1
  101.4 2.8 fusion
  104.2 0.0 collective-permute-done
  104.2 0.0 collective-permute-done.1
  104.2 4.8 fusion.16
  109.0 33.7 %all-gather.11.cloned.1.call-done = bf16[512,2048]{1,0:T(8,128)(2,1)} async-done(((bf16[512,256]{1,0:T(8,128)(2,1)}), bf16[512,2048]{1,0:T(8,128)(2,1)}) %all-gather.11.cloned.1.call-update) | async-done | bytes 2097168 | tf_op jit(solution)/shard_map/all_gather | solution.py:79
  142.7 4.4 convolution_convert_fusion
  147.1 0.0 all-reduce.2.cloned.1.call-update
  147.1 0.0 copy-start.4
  147.1 0.0 all-gather.13.cloned.1.call-start
  147.2 0.5 all-gather.13.cloned.1.call-update
  147.7 0.0 all-gather.15.cloned.1.call-start
  147.8 0.5 all-gather.15.cloned.1.call-update
  148.3 0.0 all-gather.17.cloned.1.call-start
  148.4 0.7 all-gather.17.cloned.1.call-update
  149.1 0.3 reduce-scatter.2.cloned.1.call-start
  149.3 47.5 %all-reduce.2.cloned.1.call-done = bf16[512,2048]{1,0:T(8,128)(2,1)} async-done(((bf16[512,2048]{1,0:T(8,128)(2,1)}), bf16[512,2048]{1,0:T(8,128)(2,1)}) %all-reduce.2.cloned.1.call-update) | async-done | bytes 2097168 | tf_op jit(solution)/shard_map/psum | solution.py:82
  196.9 3.9 fusion.4
  200.8 90.5 %all-gather.13.cloned.1.call-done = bf16[2048,1408]{1,0:T(8,128)(2,1)} async-done(((bf16[256,1408]{1,0:T(8,128)(2,1)}), bf16[2048,1408]{1,0:T(8,128)(2,1)}) %all-gather.13.cloned.1.call-update) | async-done | bytes 5767184 | tf_op jit(solution)/shard_map/all_gather | solution.py:88
  291.3 8.4 %fusion.21 = f32[512,1408]{1,0:T(8,128)} fusion(bf16[2048,1408]{1,0:T(8,128)(2,1)} %all-gather.13.cloned.1.call-done, bf16[512,2048]{1,0:T(8,128)(2,1)} %get-tuple-element.6, f32[2048]{0:T(1024)S(1)} %copy-done.4, f32[512]{0:T(512)S(1)} %add_rsqrt_fusion), kind=kOutput, calls=%fused_computation.33 | convolution fusion | flops 2956984320 | bytes 10758144 | tf_op jit(solution)/shard_map/dot_general | solution.py:23
  299.7 84.1 %all-gather.15.cloned.1.call-done = bf16[2048,1408]{1,0:T(8,128)(2,1)} async-done(((bf16[256,1408]{1,0:T(8,128)(2,1)}), bf16[2048,1408]{1,0:T(8,128)(2,1)}) %all-gather.15.cloned.1.call-update) | async-done | bytes 5767184 | tf_op jit(solution)/shard_map/all_gather | solution.py:89
  383.9 93.4 %all-gather.17.cloned.1.call-done = bf16[1408,2048]{1,0:T(8,128)(2,1)} async-done(((bf16[1408,256]{1,0:T(8,128)(2,1)}), bf16[1408,2048]{1,0:T(8,128)(2,1)}) %all-gather.17.cloned.1.call-update) | async-done | bytes 5767184 | tf_op jit(solution)/shard_map/all_gather | solution.py:93
  477.2 0.0 copy-done.1
  477.2 13.4 %convolution_convert_fusion.1 = bf16[512,2048]{1,0:T(8,128)(2,1)} fusion(bf16[1408,2048]{1,0:T(8,128)(2,1)} %all-gather.17.cloned.1.call-done, bf16[2048,1408]{1,0:T(8,128)(2,1)} %all-gather.15.cloned.1.call-done, f32[512,1408]{1,0:T(8,128)} %fusion.21, bf16[512,2048]{1,0:T(8,128)(2,1)S(1)} %copy-done.1, f32[2048]{0:T(1024)S(1)} %copy-done.4, ...), kind=kOutput, calls=%fused_computation.27 | convolution fusion | flops 5915148288 | bytes 18622464 | tf_op jit(solution)/shard_map/dot_general | solution.py:23
  490.7 0.0 reduce-scatter.2.cloned.1.call-update
  490.7 29.5 %reduce-scatter.2.cloned.1.call-done = bf16[512,512]{1,0:T(8,128)(2,1)} async-done(((bf16[512,2048]{1,0:T(8,128)(2,1)}), bf16[512,512]{1,0:T(8,128)(2,1)}) %reduce-scatter.2.cloned.1.call-update) | async-done | bytes 524304 | tf_op jit(solution)/shard_map/reduce_scatter | solution.py:95
  520.2 2.0 add_convert_fusion
  (13 shorter events, 0.0 us)
Async XLA Ops:
  6.5 74.4 %copy-start.3 = (f32[2048]{0:T(1024)S(1)}, f32[2048]{0:T(1024)}, u32[]{:S(2)}) copy-start(f32[2048]{0:T(1024)} %param.11) | copy-start | bytes 24580
  6.5 72.1 %all-gather.7.cloned.1.call-start = ((), (), s32[]{:S(2)}) async-start(), calls=%async_computation.1 | async-start | bytes 2621440 | tf_op jit(solution)/shard_map/all_gather | solution.py:57
  7.3 87.8 %all-gather.9.cloned.1.call-start = ((), (), s32[]{:S(2)}) async-start(), calls=%async_computation.2 | async-start | bytes 2359296 | tf_op jit(solution)/shard_map/all_gather | solution.py:59
  8.0 134.7 %all-gather.11.cloned.1.call-start = ((), (), s32[]{:S(2)}) async-start(), calls=%async_computation.3 | async-start | bytes 2359296 | tf_op jit(solution)/shard_map/all_gather | solution.py:79
  8.7 188.1 %all-reduce.2.cloned.1.call-start = ((), (), s32[]{:S(2)}) async-start(), calls=%async_computation.4 | async-start | bytes 4194304 | tf_op jit(solution)/shard_map/psum | solution.py:82
  78.6 10.2 %copy-start = (bf16[512,2048]{1,0:T(8,128)(2,1)S(1)}, bf16[512,2048]{1,0:T(8,128)(2,1)}, u32[]{:S(2)}) copy-start(bf16[512,2048]{1,0:T(8,128)(2,1)} %all-gather.7.cloned.1.call-done) | copy-start | bytes 6291460
  78.7 10.2 %copy-start.2 = (bf16[2048,128]{1,0:T(8,128)(2,1)S(1)}, bf16[2048,128]{1,0:T(8,128)(2,1)}, u32[]{:S(2)}) copy-start(bf16[2048,128]{1,0:T(8,128)(2,1)} %all_gather.25) | copy-start | bytes 1572868
  83.3 14.8 %collective-permute-start.2 = (bf16[512,128]{1,0:T(8,128)(2,1)S(1)}, bf16[512,128]{1,0:T(8,128)(2,1)S(1)}, u32[]{:S(2)}, u32[]{:S(2)}) collective-permute-start(bf16[512,128]{1,0:T(8,128)(2,1)S(1)} %convolution_convert_fusion.3), channel_id=1, source_target_pairs={{0,8},{4,12},{8,16},{12,20},{16,24},{20,28},{1,9},{5,13},{9,17},{1... | collective-permute-start | bytes 393224 | tf_op jit(solution)/shard_map/ppermute | solution.py:13
  84.6 13.5 %collective-permute-start.3 = (bf16[512,128]{1,0:T(8,128)(2,1)S(1)}, bf16[512,128]{1,0:T(8,128)(2,1)}, u32[]{:S(2)}, u32[]{:S(2)}) collective-permute-start(bf16[512,128]{1,0:T(8,128)(2,1)S(1)} %convolution_convert_fusion.3), channel_id=1, source_target_pairs={{0,4},{4,8},{8,12},{12,16},{16,20},{20,24},{24,28},{1,5},{5,9},{9,... | collective-permute-start | bytes 393224 | tf_op jit(solution)/shard_map/ppermute | solution.py:13
  89.6 14.5 %collective-permute-start = (bf16[512,128]{1,0:T(8,128)(2,1)S(1)}, bf16[512,128]{1,0:T(8,128)(2,1)S(1)}, u32[]{:S(2)}, u32[]{:S(2)}) collective-permute-start(bf16[512,128]{1,0:T(8,128)(2,1)S(1)} %convolution_convert_fusion.4), channel_id=1, source_target_pairs={{0,8},{4,12},{8,16},{12,20},{16,24},{20,28},{1,9},{5,13},{9,17},{1... | collective-permute-start | bytes 393224 | tf_op jit(solution)/shard_map/ppermute | solution.py:13
  92.4 11.8 %collective-permute-start.1 = (bf16[512,128]{1,0:T(8,128)(2,1)S(1)}, bf16[512,128]{1,0:T(8,128)(2,1)S(1)}, u32[]{:S(2)}, u32[]{:S(2)}) collective-permute-start(bf16[512,128]{1,0:T(8,128)(2,1)S(1)} %convolution_convert_fusion.4), channel_id=1, source_target_pairs={{0,4},{4,8},{8,12},{12,16},{16,20},{20,24},{24,28},{1,5},{5,9},{9,... | collective-permute-start | bytes 393224 | tf_op jit(solution)/shard_map/ppermute | solution.py:13
  147.1 144.2 %copy-start.4 = (f32[2048]{0:T(1024)S(1)}, f32[2048]{0:T(1024)}, u32[]{:S(2)}) copy-start(f32[2048]{0:T(1024)} %param.16) | copy-start | bytes 24580
  147.1 144.1 %all-gather.13.cloned.1.call-start = ((), (), s32[]{:S(2)}) async-start(), calls=%async_computation.5 | async-start | bytes 6488064 | tf_op jit(solution)/shard_map/all_gather | solution.py:88
  147.7 236.1 %all-gather.15.cloned.1.call-start = ((), (), s32[]{:S(2)}) async-start(), calls=%async_computation.6 | async-start | bytes 6488064 | tf_op jit(solution)/shard_map/all_gather | solution.py:89
  148.3 328.9 %all-gather.17.cloned.1.call-start = ((), (), s32[]{:S(2)}) async-start(), calls=%async_computation.7 | async-start | bytes 6488064 | tf_op jit(solution)/shard_map/all_gather | solution.py:93
  149.1 371.1 %reduce-scatter.2.cloned.1.call-start = ((), (), s32[]{:S(2)}) async-start(), calls=%async_computation.8 | async-start | bytes 2621440 | tf_op jit(solution)/shard_map/reduce_scatter | solution.py:95
  291.3 185.9 %copy-start.1 = (bf16[512,2048]{1,0:T(8,128)(2,1)S(1)}, bf16[512,2048]{1,0:T(8,128)(2,1)}, u32[]{:S(2)}) copy-start(bf16[512,2048]{1,0:T(8,128)(2,1)} %get-tuple-element.6) | copy-start | bytes 6291460
Sparse Core Ops, SparseCore 0:
  8.9 25.2 all-gather.6
  36.3 52.5 all-gather.8
  91.0 51.7 all-gather.10
  147.3 49.5 all-reduce.1
  198.9 92.3 all-gather.12
  293.3 90.4 all-gather.14
  385.9 91.2 all-gather.16
  490.8 29.3 reduce-scatter.1
where the time goes:
time: 529 us
  waiting for transfers between devices  383 us (72%)
  blocking collectives  68.5 us (13%)
  matrix products  40.5 us (8%)
  between operations  13.7 us (3%)
  other arithmetic  12.2 us (2%)
  starting transfers between devices  11.5 us (2%)
    all_gather x1, waiting for transfers between devices, per_device(): down_full = lax.all_gather(w_down, 'seq', axis=1, tiled=True)  93.4 us
    all_gather x1, waiting for transfers between devices, per_device(): gate_full = lax.all_gather(w_gate, 'seq', axis=0, tiled=True)  90.5 us
    all_gather x1, waiting for transfers between devices, per_device(): up_full = lax.all_gather(w_up, 'seq', axis=0, tiled=True)  84.1 us
    psum x1, waiting for transfers between devices, per_device(): lax.psum(head_terms.astype(jnp.bfloat16), 'tensor').astype(jnp.float32)  47.5 us
    all_gather x1, blocking collectives, per_device(): lax.all_gather(w_value, 'seq', axis=0, tiled=True)  35.2 us
    all_gather x1, waiting for transfers between devices, per_device(): out_full = lax.all_gather(w_out, 'seq', axis=1, tiled=True)  33.7 us
    all_gather x1, blocking collectives, per_device(): lax.all_gather(w_key, 'seq', axis=0, tiled=True)  33.4 us
    dot_general x6, matrix products, product(): return jnp.dot(left, right, preferred_element_type=jnp.float32)  32.3 us
  transfers between devices with their start and end apart: 12, of which 6 were waited for; matrix products, arithmetic and copies ran while one was open for 6% of the time, Pallas kernels for 0%

commit v1 on v0

--- a/solution.py
+++ b/solution.py
@@ -90,7 +90,7 @@
     gate = product(stream_normed, gate_full)
     upward = product(stream_normed, up_full)
     hidden = (jax.nn.silu(gate) * upward).astype(jnp.bfloat16)
-    down_full = lax.all_gather(w_down, "seq", axis=1, tiled=True)
+    down_full = jnp.concatenate(lax.all_gather(w_down, "seq"), axis=1)
     unit_terms = product(hidden, down_full)
     mlp_share = lax.psum_scatter(
         unit_terms.astype(jnp.bfloat16), "tensor", scatter_dimension=1, tiled=True

time: 529 us -> 529 us (level)
  waiting for transfers between devices: 383 us -> 374 us
  local copies, waits for them, and re-layouts: 0.02 us -> 8.38 us
    reshape x0 -> x1, local copies, waits for them, and re-layouts: none -> 8.36 us  [per_device(): down_full = jnp.concatenate(lax.all_gather(w_down, 'seq'), axis=1)]
    all_gather x1, waiting for transfers between devices: 90.5 us -> 84.2 us  [per_device(): gate_full = lax.all_gather(w_gate, 'seq', axis=0, tiled=True)]
  transfers between devices with their start and end apart: 12 -> 12, of which waited for: 6 -> 6; matrix products, arithmetic and copies ran while one was open for 6% -> 8% of each run, Pallas kernels for 0% -> 0%
where the time goes in v1:
time: 529 us; the launch traced here: 528 us
  waiting for transfers between devices  374 us (71%)
  blocking collectives  68.5 us (13%)
  matrix products  39.6 us (7%)
  between operations  13.6 us (3%)
  other arithmetic  12.2 us (2%)
  starting transfers between devices  11.5 us (2%)
  local copies, waits for them, and re-layouts  8.38 us (2%)
    all_gather x1, waiting for transfers between devices, per_device(): down_full = jnp.concatenate(lax.all_gather(w_down, 'seq'), axis=1)  90.5 us
    all_gather x1, waiting for transfers between devices, per_device(): up_full = lax.all_gather(w_up, 'seq', axis=0, tiled=True)  85 us
    all_gather x1, waiting for transfers between devices, per_device(): gate_full = lax.all_gather(w_gate, 'seq', axis=0, tiled=True)  84.2 us
    psum x1, waiting for transfers between devices, per_device(): lax.psum(head_terms.astype(jnp.bfloat16), 'tensor').astype(jnp.float32)  47.5 us
    all_gather x1, blocking collectives, per_device(): lax.all_gather(w_value, 'seq', axis=0, tiled=True)  35.2 us
    all_gather x1, waiting for transfers between devices, per_device(): out_full = lax.all_gather(w_out, 'seq', axis=1, tiled=True)  33.7 us
    all_gather x1, blocking collectives, per_device(): lax.all_gather(w_key, 'seq', axis=0, tiled=True)  33.4 us
    dot_general x6, matrix products, product(): return jnp.dot(left, right, preferred_element_type=jnp.float32)  31.5 us
  transfers between devices with their start and end apart: 12, of which 6 were waited for; matrix products, arithmetic and copies ran while one was open for 8% of the time, Pallas kernels for 0%

profile of v1, /device:TPU:0, one launch (start us, length us, event | category | flops | bytes accessed | tf_op | source)
XLA Modules:
  0.0 528.2 jit_solution(10851936127894093240)
XLA Ops:
  6.5 0.7 all-gather.8.cloned.1.call-update
  7.3 0.0 all-gather.10.cloned.1.call-start
  7.3 0.7 all-gather.10.cloned.1.call-update
  8.0 0.0 all-gather.12.cloned.1.call-start
  8.1 0.7 all-gather.12.cloned.1.call-update
  8.7 0.0 all-reduce.2.cloned.1.call-start
  8.8 33.4 %all_gather.29 = bf16[2048,128]{1,0:T(8,128)(2,1)S(1)} all-gather(bf16[256,128]{1,0:T(8,128)(2,1)} %param.13), channel_id=1, replica_groups=mesh['seq'=8,'tensor'=4] {'seq'}, dimensions={0}, use_global_device_ids=true | all-gather | bytes 589824 | tf_op jit(solution)/shard_map/all_gather | solution.py:61
  42.2 35.2 %all_gather.28 = bf16[2048,128]{1,0:T(8,128)(2,1)} all-gather(bf16[256,128]{1,0:T(8,128)(2,1)} %param.14), channel_id=1, replica_groups=mesh['seq'=8,'tensor'=4] {'seq'}, dimensions={0}, use_global_device_ids=true | all-gather | bytes 589824 | tf_op jit(solution)/shard_map/all_gather | solution.py:62
  77.3 1.3 fusion.14
  78.6 0.0 all-gather.8.cloned.1.call-done
  78.7 2.2 fusion.7
  80.9 2.4 convolution_convert_fusion.3
  83.3 1.3 collective-permute-start.2
  84.6 4.3 collective-permute-start.3
  88.9 0.8 convolution_convert_fusion.4
  89.6 2.7 collective-permute-start
  92.4 2.7 collective-permute-start.1
  95.1 0.0 all-gather.10.cloned.1.call-done
  95.1 3.0 convolution_convert_fusion.2
  98.1 0.0 collective-permute-done.2
  98.1 0.0 collective-permute-done.3
  98.1 3.3 fusion.1
  101.4 2.8 fusion
  104.2 0.0 collective-permute-done
  104.2 0.0 collective-permute-done.1
  104.2 4.8 fusion.16
  109.0 33.7 %all-gather.12.cloned.1.call-done = bf16[512,2048]{1,0:T(8,128)(2,1)} async-done(((bf16[512,256]{1,0:T(8,128)(2,1)}), bf16[512,2048]{1,0:T(8,128)(2,1)}) %all-gather.12.cloned.1.call-update) | async-done | bytes 2097168 | tf_op jit(solution)/shard_map/all_gather | solution.py:79
  142.7 4.4 convolution_convert_fusion
  147.1 0.0 all-reduce.2.cloned.1.call-update
  147.1 0.0 all-gather.18.cloned.1.call-start
  147.2 0.5 all-gather.18.cloned.1.call-update
  147.7 0.0 all-gather.14.cloned.1.call-start
  147.8 0.5 all-gather.14.cloned.1.call-update
  148.3 0.0 all-gather.16.cloned.1.call-start
  148.3 0.7 all-gather.16.cloned.1.call-update
  149.1 0.3 reduce-scatter.2.cloned.1.call-start
  149.3 47.5 %all-reduce.2.cloned.1.call-done = bf16[512,2048]{1,0:T(8,128)(2,1)} async-done(((bf16[512,2048]{1,0:T(8,128)(2,1)}), bf16[512,2048]{1,0:T(8,128)(2,1)}) %all-reduce.2.cloned.1.call-update) | async-done | bytes 2097168 | tf_op jit(solution)/shard_map/psum | solution.py:82
  196.9 3.9 fusion.4
  200.8 90.5 %all-gather.18.cloned.1.call-done = bf16[11264,256]{1,0:T(8,128)(2,1)} async-done(((bf16[1408,256]{1,0:T(8,128)(2,1)}), bf16[11264,256]{1,0:T(8,128)(2,1)}) %all-gather.18.cloned.1.call-update) | async-done | bytes 5767184 | tf_op jit(solution)/shard_map/all_gather | solution.py:93
  291.3 8.4 %copy.20 = bf16[1408,8,256]{0,2,1:T(8,128)(2,1)} copy(bf16[1408,8,256]{2,0,1:T(8,128)(2,1)} %bitcast.47) | data formatting | bytes 11534336 | tf_op jit(solution)/shard_map/reshape | solution.py:93
  299.7 84.2 %all-gather.14.cloned.1.call-done = bf16[2048,1408]{1,0:T(8,128)(2,1)} async-done(((bf16[256,1408]{1,0:T(8,128)(2,1)}), bf16[2048,1408]{1,0:T(8,128)(2,1)}) %all-gather.14.cloned.1.call-update) | async-done | bytes 5767184 | tf_op jit(solution)/shard_map/all_gather | solution.py:88
  383.9 0.0 copy-done.1
  383.9 7.7 %fusion.21 = f32[512,1408]{1,0:T(8,128)} fusion(bf16[2048,1408]{1,0:T(8,128)(2,1)} %all-gather.14.cloned.1.call-done, bf16[512,2048]{1,0:T(8,128)(2,1)S(1)} %copy-done.1, f32[2048]{0:T(1024)S(1)} %copy-done.4, f32[512]{0:T(512)S(1)} %add_rsqrt_fusion), kind=kOutput, calls=%fused_computation.33 | convolution fusion | flops 2956984320 | bytes 10758144 | tf_op jit(solution)/shard_map/dot_general | solution.py:23
  391.6 85.0 %all-gather.16.cloned.1.call-done = bf16[2048,1408]{1,0:T(8,128)(2,1)} async-done(((bf16[256,1408]{1,0:T(8,128)(2,1)}), bf16[2048,1408]{1,0:T(8,128)(2,1)}) %all-gather.16.cloned.1.call-update) | async-done | bytes 5767184 | tf_op jit(solution)/shard_map/all_gather | solution.py:89
  476.6 13.3 %convolution_convert_fusion.1 = bf16[512,2048]{1,0:T(8,128)(2,1)} fusion(bf16[1408,2048]{0,1:T(8,128)(2,1)} %bitcast.48, bf16[2048,1408]{1,0:T(8,128)(2,1)} %all-gather.16.cloned.1.call-done, f32[512,1408]{1,0:T(8,128)} %fusion.21, bf16[512,2048]{1,0:T(8,128)(2,1)S(1)} %copy-done.1, f32[2048]{0:T(1024)S(1)} %copy-done.4, f32[512]{0:T(512)S(1)} %add_rsqrt_fusion), kind=kOutput, calls=%fused_computation.27 | convolution fusion | flops 5915148288 | bytes 18622464 | tf_op jit(solution)/shard_map/dot_general | solution.py:23
  489.8 0.0 reduce-scatter.2.cloned.1.call-update
  489.9 29.5 %reduce-scatter.2.cloned.1.call-done = bf16[512,512]{1,0:T(8,128)(2,1)} async-done(((bf16[512,2048]{1,0:T(8,128)(2,1)}), bf16[512,512]{1,0:T(8,128)(2,1)}) %reduce-scatter.2.cloned.1.call-update) | async-done | bytes 524304 | tf_op jit(solution)/shard_map/reduce_scatter | solution.py:95
  519.3 2.0 add_convert_fusion
  (14 shorter events, 0.0 us)
Async XLA Ops:
  6.5 74.4 %copy-start.3 = (f32[2048]{0:T(1024)S(1)}, f32[2048]{0:T(1024)}, u32[]{:S(2)}) copy-start(f32[2048]{0:T(1024)} %param.11) | copy-start | bytes 24580
  6.5 72.1 %all-gather.8.cloned.1.call-start = ((), (), s32[]{:S(2)}) async-start(), calls=%async_computation.1 | async-start | bytes 2621440 | tf_op jit(solution)/shard_map/all_gather | solution.py:57
  7.3 87.8 %all-gather.10.cloned.1.call-start = ((), (), s32[]{:S(2)}) async-start(), calls=%async_computation.2 | async-start | bytes 2359296 | tf_op jit(solution)/shard_map/all_gather | solution.py:59
  8.0 134.7 %all-gather.12.cloned.1.call-start = ((), (), s32[]{:S(2)}) async-start(), calls=%async_computation.3 | async-start | bytes 2359296 | tf_op jit(solution)/shard_map/all_gather | solution.py:79
  8.7 188.1 %all-reduce.2.cloned.1.call-start = ((), (), s32[]{:S(2)}) async-start(), calls=%async_computation.4 | async-start | bytes 4194304 | tf_op jit(solution)/shard_map/psum | solution.py:82
  78.6 10.2 %copy-start = (bf16[512,2048]{1,0:T(8,128)(2,1)S(1)}, bf16[512,2048]{1,0:T(8,128)(2,1)}, u32[]{:S(2)}) copy-start(bf16[512,2048]{1,0:T(8,128)(2,1)} %all-gather.8.cloned.1.call-done) | copy-start | bytes 6291460
  78.7 10.2 %copy-start.2 = (bf16[2048,128]{1,0:T(8,128)(2,1)S(1)}, bf16[2048,128]{1,0:T(8,128)(2,1)}, u32[]{:S(2)}) copy-start(bf16[2048,128]{1,0:T(8,128)(2,1)} %all_gather.28) | copy-start | bytes 1572868
  83.3 14.8 %collective-permute-start.2 = (bf16[512,128]{1,0:T(8,128)(2,1)S(1)}, bf16[512,128]{1,0:T(8,128)(2,1)S(1)}, u32[]{:S(2)}, u32[]{:S(2)}) collective-permute-start(bf16[512,128]{1,0:T(8,128)(2,1)S(1)} %convolution_convert_fusion.3), channel_id=1, source_target_pairs={{0,8},{4,12},{8,16},{12,20},{16,24},{20,28},{1,9},{5,13},{9,17},{1... | collective-permute-start | bytes 393224 | tf_op jit(solution)/shard_map/ppermute | solution.py:13
  84.6 13.5 %collective-permute-start.3 = (bf16[512,128]{1,0:T(8,128)(2,1)S(1)}, bf16[512,128]{1,0:T(8,128)(2,1)}, u32[]{:S(2)}, u32[]{:S(2)}) collective-permute-start(bf16[512,128]{1,0:T(8,128)(2,1)S(1)} %convolution_convert_fusion.3), channel_id=1, source_target_pairs={{0,4},{4,8},{8,12},{12,16},{16,20},{20,24},{24,28},{1,5},{5,9},{9,... | collective-permute-start | bytes 393224 | tf_op jit(solution)/shard_map/ppermute | solution.py:13
  89.6 14.5 %collective-permute-start = (bf16[512,128]{1,0:T(8,128)(2,1)S(1)}, bf16[512,128]{1,0:T(8,128)(2,1)S(1)}, u32[]{:S(2)}, u32[]{:S(2)}) collective-permute-start(bf16[512,128]{1,0:T(8,128)(2,1)S(1)} %convolution_convert_fusion.4), channel_id=1, source_target_pairs={{0,8},{4,12},{8,16},{12,20},{16,24},{20,28},{1,9},{5,13},{9,17},{1... | collective-permute-start | bytes 393224 | tf_op jit(solution)/shard_map/ppermute | solution.py:13
  92.4 11.8 %collective-permute-start.1 = (bf16[512,128]{1,0:T(8,128)(2,1)S(1)}, bf16[512,128]{1,0:T(8,128)(2,1)S(1)}, u32[]{:S(2)}, u32[]{:S(2)}) collective-permute-start(bf16[512,128]{1,0:T(8,128)(2,1)S(1)} %convolution_convert_fusion.4), channel_id=1, source_target_pairs={{0,4},{4,8},{8,12},{12,16},{16,20},{20,24},{24,28},{1,5},{5,9},{9,... | collective-permute-start | bytes 393224 | tf_op jit(solution)/shard_map/ppermute | solution.py:13
  147.1 144.2 %all-gather.18.cloned.1.call-start = ((), (), s32[]{:S(2)}) async-start(), calls=%async_computation.8 | async-start | bytes 6488064 | tf_op jit(solution)/shard_map/all_gather | solution.py:93
  147.7 236.1 %all-gather.14.cloned.1.call-start = ((), (), s32[]{:S(2)}) async-start(), calls=%async_computation.5 | async-start | bytes 6488064 | tf_op jit(solution)/shard_map/all_gather | solution.py:88
  148.3 328.3 %all-gather.16.cloned.1.call-start = ((), (), s32[]{:S(2)}) async-start(), calls=%async_computation.6 | async-start | bytes 6488064 | tf_op jit(solution)/shard_map/all_gather | solution.py:89
  149.1 370.3 %reduce-scatter.2.cloned.1.call-start = ((), (), s32[]{:S(2)}) async-start(), calls=%async_computation.7 | async-start | bytes 2621440 | tf_op jit(solution)/shard_map/reduce_scatter | solution.py:95
  291.3 92.6 %copy-start.1 = (bf16[512,2048]{1,0:T(8,128)(2,1)S(1)}, bf16[512,2048]{1,0:T(8,128)(2,1)}, u32[]{:S(2)}) copy-start(bf16[512,2048]{1,0:T(8,128)(2,1)} %get-tuple-element.6) | copy-start | bytes 6291460
  291.3 92.6 %copy-start.4 = (f32[2048]{0:T(1024)S(1)}, f32[2048]{0:T(1024)}, u32[]{:S(2)}) copy-start(f32[2048]{0:T(1024)} %param.16) | copy-start | bytes 24580
Sparse Core Ops, SparseCore 0:
  8.9 25.2 all-gather.7
  36.3 52.5 all-gather.9
  91.0 51.7 all-gather.11
  147.3 49.5 all-reduce.1
  198.9 92.3 all-gather.17
  293.3 90.4 all-gather.13
  386.0 90.4 all-gather.15
  490.0 29.3 reduce-scatter.1
